TPU v7x, 32 devices: a whole 2x2x4 slice. The times are simulated.
32 devices in a mesh: freq: 4 (over y, core), lat: 8 (over z, x).
Axes of the slice: x: 2, y: 2, z: 4, core: 2. Of those that a mesh axis runs over, the one named last changes fastest.
Arguments:
- spectra: float32 [2, 4, 32768], P(None, None, ('freq', 'lat')), may hold values from -6 to 6
- tile_route: int32 [32768, 1], P(('freq', 'lat')), may hold values from 0 to 255; in each aligned block of 1024 rows (0 to 1023, 1024 to 2047, ...) at most 8 rows name the same one
- bin_in_tile: int32 [32768], P(('freq', 'lat')), may hold values from 0 to 1023
- trace_offset: float32 [2, 32768], P(None, ('freq', 'lat')), may hold values from -0.5 to 0.5
- weights: float32 [32768], P(('freq', 'lat')), may hold values from 0.2 to 5
- frequency: float32 [4], P('freq'), may hold values from 0.5 to 1.5
- slowness: float32 [2, 8], replicated, may hold values from 0.6 to 1.6
- vel_index: int32 [2, 512, 512], P(None, 'lat'), may hold values from 0 to 7
Outputs:
- wavefield: float32 [2, 4, 512, 512], P(None, 'freq', 'lat')
- depth_image: float32 [2, 512, 512], P(None, 'lat', 'freq')
Inputs may be any that keep to these rules, and one draw needn't show every extreme that they name: `tile_route`: tiles of 32 x 32 bins, numbered row by row over the grid; among the rows of one device no tile is named by more than 8 traces. `bin_in_tile`: row * 32 + column of the bin within the tile.
All inputs are finite; a program needn't handle non-finite values.
Results may differ from a plain program's by a relative error of at most 0.0003.
Values sent between devices are 32-bit elements; how exact they have to be, the bound alone decides.
A program may use at most 64 MiB of HBM per device.

v0:
```python
import math

import jax
import jax.numpy as jnp
from jax import lax
from jax.sharding import PartitionSpec as P

NX = 512
NY = 512
TB = 32
MODES = 8
NSTEPS = 2
NREF = 2
NVEL = 8
TILES = 256
CAP = 8


damping = 1.0
depth_step = 1.0
block_tiles = 8


def dft_real(length, direction):
    counter = jnp.arange(length)
    angles = (
        2.0 * math.pi / length * (counter[:, None] * counter[None, :] % length).astype(jnp.float32)
    )
    cosine = jnp.cos(angles)
    sine_part = direction * jnp.sin(angles)
    return jnp.stack([jnp.stack([cosine, sine_part], 1), jnp.stack([-sine_part, cosine], 1)], 0)


def twiddle(full_length, first_len, second_len, direction):
    first_at = jnp.arange(first_len)[:, None]
    second_at = jnp.arange(second_len)[None, :]
    angles = 2.0 * math.pi / full_length * (first_at * second_at % full_length).astype(jnp.float32)
    return (jnp.cos(angles), direction * jnp.sin(angles))


def complex_scale(values, cosine, sine_part, part_axis):
    real_part = jnp.take(values, 0, axis=part_axis)
    imag_part = jnp.take(values, 1, axis=part_axis)
    return jnp.stack(
        [real_part * cosine - imag_part * sine_part, real_part * sine_part + imag_part * cosine],
        part_axis,
    )


def normal_terms(trace_meta, values_in):
    slot_count = trace_meta.shape[-1]
    tile_count = slot_count // CAP
    block_width = block_tiles * CAP
    mode_ids = jnp.arange(MODES).astype(jnp.float32)[:, None, None, None, None]

    def one_block(block_at):
        meta_part = lax.dynamic_slice_in_dim(trace_meta, block_at * block_width, block_width, 4)
        data_part = lax.dynamic_slice_in_dim(values_in, block_at * block_width, block_width, 4)
        meta_part = meta_part.reshape(meta_part.shape[:4] + (block_tiles, CAP))
        data_part = data_part.reshape(data_part.shape[:4] + (block_tiles, CAP))
        weight_part = meta_part[0, :, 0]
        along_x = jnp.cos(math.pi * mode_ids * (meta_part[1, :, 0][None] + 0.5) / TB)
        along_y = jnp.cos(math.pi * mode_ids * (meta_part[2, :, 0][None] + 0.5) / TB)
        basis_vals = (along_x[:, None] * along_y[None, :]).reshape(
            (MODES * MODES,) + weight_part.shape
        )
        weighted = basis_vals * weight_part[None]
        normal = jnp.einsum(
            "iabgc,jabgc->gij", weighted, basis_vals, precision=lax.Precision.HIGHEST
        )
        right_side = jnp.einsum(
            "iabgc,paqbgc->gipq", weighted, data_part, precision=lax.Precision.HIGHEST
        )
        return (normal, right_side)

    normal, right_side = lax.map(one_block, jnp.arange(tile_count // block_tiles))
    normal = normal.reshape(tile_count, MODES * MODES, MODES * MODES)
    right_side = right_side.reshape((tile_count, MODES * MODES) + right_side.shape[3:])
    return (normal, right_side)


def fit_grid(normal, right_side, row_count):
    tile_count = normal.shape[0]
    system = normal + damping * jnp.eye(MODES * MODES, dtype=jnp.float32)
    factor = jnp.linalg.cholesky(system)
    flat_rhs = right_side.reshape(tile_count, MODES * MODES, -1)
    middle = jax.scipy.linalg.solve_triangular(factor, flat_rhs, lower=True)
    coeffs = jax.scipy.linalg.solve_triangular(factor, middle, lower=True, trans="T")
    coeffs = coeffs.reshape(row_count // TB, NY // TB, MODES, MODES, 2, -1)
    cell_pos = jnp.arange(TB).astype(jnp.float32)
    cos_table = jnp.cos(
        math.pi * jnp.arange(MODES).astype(jnp.float32)[:, None] * (cell_pos[None, :] + 0.5) / TB
    )
    viewed = jnp.einsum(
        "xyabpq,ai,bj->pqxiyj", coeffs, cos_table, cos_table, precision=lax.Precision.HIGHEST
    )
    return viewed.reshape(2, viewed.shape[1], row_count, NY)


def local(spectra, tile_route, bin_in_tile, trace_offset, weights, frequency, slowness, vel_index):
    lat_count = lax.axis_size("lat")
    row_count = vel_index.shape[1]
    tile_dev = TILES // lat_count
    slot_count = tile_dev * CAP
    total_freqs = spectra.shape[1]
    tile_id = tile_route[:, 0]
    trace_count = tile_id.shape[0]
    ranking = jnp.argsort(tile_id, stable=True)
    sorted_tiles = tile_id[ranking]
    firsts = jnp.searchsorted(sorted_tiles, sorted_tiles, side="left")
    position = sorted_tiles * CAP + jnp.arange(trace_count, dtype=jnp.int32) - firsts
    slot_of = jnp.zeros((trace_count,), jnp.int32).at[ranking].set(position)
    owner_lat = slot_of // slot_count
    within = slot_of % slot_count
    cell_x = (bin_in_tile // TB).astype(jnp.float32) + trace_offset[0]
    cell_y = (bin_in_tile % TB).astype(jnp.float32) + trace_offset[1]
    trace_meta = jnp.stack([weights, cell_x, cell_y], 0)
    meta_buf = (
        jnp.zeros((3, lat_count, slot_count), jnp.float32).at[:, owner_lat, within].set(trace_meta)
    )
    spec_buf = (
        jnp.zeros((2, total_freqs, lat_count, slot_count), jnp.float32)
        .at[:, :, owner_lat, within]
        .set(spectra)
    )
    got_spec, got_meta = (
        lax.all_to_all(spec_buf, "lat", split_axis=2, concat_axis=2, tiled=True),
        lax.all_to_all(meta_buf[:, None], "lat", split_axis=2, concat_axis=2, tiled=True),
    )
    normal, right_side = normal_terms(got_meta[:, None], got_spec[:, None])
    normal = lax.psum(normal, "freq")
    right_side = lax.psum_scatter(right_side, "freq", scatter_dimension=3, tiled=True)
    wave_field = fit_grid(normal, right_side, row_count)
    len_x = NX // 8
    len_y = NY // 8
    w8_fwd = dft_real(8, -1.0)
    w8_inv = dft_real(8, 1.0)
    wx_fwd = dft_real(len_x, -1.0)
    wx_inv = dft_real(len_x, 1.0)
    wy_fwd = dft_real(len_y, -1.0)
    wy_inv = dft_real(len_y, 1.0)
    twx_fwd = twiddle(NX, 8, len_x, -1.0)
    twx_inv = twiddle(NX, 8, len_x, 1.0)
    twy_fwd = twiddle(NY, 8, len_y, -1.0)
    twy_inv = twiddle(NY, 8, len_y, 1.0)
    inverse_scale = 1.0 / (NX * NY)

    def forward_x(columns):
        dims_of = columns.shape
        viewed = columns.reshape(dims_of[:4] + (8, len_x))
        section_a = jnp.einsum(
            "phkqmn,pmsl->shkqln", viewed, w8_fwd, precision=lax.Precision.HIGHEST
        )
        section_b = complex_scale(section_a, twx_fwd[0], twx_fwd[1], 0)
        return jnp.einsum("shkqln,snto->thkqlo", section_b, wx_fwd, precision=lax.Precision.HIGHEST)

    def inverse_y(columns):
        section_c = jnp.einsum(
            "jthkqr,thsn->jsqrkn", columns, wy_inv, precision=lax.Precision.HIGHEST
        )
        section_b = complex_scale(section_c, twy_inv[0], twy_inv[1], 1)
        section_a = jnp.einsum(
            "jsqrkn,skpm->jpqrmn", section_b, w8_inv, precision=lax.Precision.HIGHEST
        )
        return section_a.reshape(section_a.shape[:4] + (NY,)) * inverse_scale

    lat_at = lax.axis_index("lat")
    ky_band = len_y // lat_count
    ky_index = jnp.arange(8)[None, :] + 8 * (lat_at * ky_band + jnp.arange(ky_band)[:, None])
    ky_signed = jnp.where(ky_index >= NY // 2, ky_index - NY, ky_index)
    ky_vals = 2.0 * math.pi / NY * ky_signed.astype(jnp.float32)
    kx_index = jnp.arange(8)[:, None] + 8 * jnp.arange(len_x)[None, :]
    kx_signed = jnp.where(kx_index >= NX // 2, kx_index - NX, kx_index)
    kx_vals = 2.0 * math.pi / NX * kx_signed.astype(jnp.float32)
    ky_sq = (ky_vals * ky_vals)[None, :, :, None, None, None]
    kx_sq = (kx_vals * kx_vals)[None, None, None, None, :, :]
    per_group = NVEL // NREF
    image_rows = []
    for depth_at in range(NSTEPS):
        table_row = slowness[depth_at]
        references = table_row.reshape(NREF, per_group).mean(axis=1)
        forward_dims_of = wave_field.shape
        forward_viewed = wave_field.reshape(forward_dims_of[:3] + (8, len_y))
        forward_section_a = jnp.einsum(
            "pqrmn,pmsk->sqrkn", forward_viewed, w8_fwd, precision=lax.Precision.HIGHEST
        )
        forward_section_b = complex_scale(forward_section_a, twy_fwd[0], twy_fwd[1], 0)
        spectrum_y = jnp.einsum(
            "sqrkn,snth->thkqr", forward_section_b, wy_fwd, precision=lax.Precision.HIGHEST
        )
        spectrum = forward_x(
            lax.all_to_all(spectrum_y, "lat", split_axis=1, concat_axis=4, tiled=True)
        )
        wave_num = frequency[None, :] * references[:, None]
        vertical = (wave_num * wave_num)[:, None, None, :, None, None] - kx_sq - ky_sq
        phase_angle = jnp.sqrt(jnp.maximum(vertical, 0.0)) * depth_step
        damped = jnp.exp(-jnp.sqrt(jnp.maximum(-vertical, 0.0)) * depth_step)
        shifted = complex_scale(
            spectrum[None], damped * jnp.cos(phase_angle), damped * jnp.sin(phase_angle), 1
        )
        inverse_section_c = jnp.einsum(
            "jthkqlo,tosn->jshkqln", shifted, wx_inv, precision=lax.Precision.HIGHEST
        )
        inverse_section_b = complex_scale(inverse_section_c, twx_inv[0], twx_inv[1], 1)
        inverse_section_a = jnp.einsum(
            "jshkqln,slpm->jphkqmn", inverse_section_b, w8_inv, precision=lax.Precision.HIGHEST
        )
        columns = inverse_section_a.reshape(inverse_section_a.shape[:5] + (NX,))
        returned = inverse_y(
            lax.all_to_all(columns, "lat", split_axis=5, concat_axis=2, tiled=True)
        )
        velocity = vel_index[depth_at]
        picked = velocity[None] == jnp.arange(NVEL)[:, None, None]
        local_slow = jnp.sum(jnp.where(picked, table_row[:, None, None], 0.0), 0)
        group_of = velocity // per_group
        split_phase = (
            frequency[None, :, None, None]
            * (local_slow[None, None] - references[:, None, None, None])
            * depth_step
        )
        group_mask = (group_of[None] == jnp.arange(NREF)[:, None, None]).astype(jnp.float32)
        corrected = complex_scale(returned, jnp.cos(split_phase), jnp.sin(split_phase), 1)
        wave_field = jnp.sum(corrected * group_mask[:, None, None], 0)
        summed = jnp.sum(wave_field[0], 0)
        image_rows.append(lax.psum_scatter(summed, "freq", scatter_dimension=1, tiled=True))
    depth_image = jnp.stack(image_rows, 0)
    return (wave_field, depth_image)


def solution(mesh):
    return jax.shard_map(
        local,
        mesh=mesh,
        in_specs=(
            P(None, None, ("freq", "lat")),
            P(("freq", "lat"), None),
            P(("freq", "lat")),
            P(None, ("freq", "lat")),
            P(("freq", "lat")),
            P("freq"),
            P(),
            P(None, "lat", None),
        ),
        out_specs=(P(None, "freq", "lat", None), P(None, "lat", "freq")),
        check_vma=False,
    )
```

profile of v0, /device:TPU:0, one launch (start us, length us, event | category | flops | bytes accessed | tf_op | source)
XLA Modules:
  0.0 646.6 jit_solution(14288893780096186821)
XLA Ops:
  7.2 5.1 sort.17
  16.9 50.7 %while.52 = (s32[]{:T(128)}, u32[1024]{0:T(1024)S(1)}, u32[1024]{0:T(1024)S(1)}, s32[1024]{0:T(1024)S(1)}, s32[]{:T(128)}, /*index=5*/s32[]{:T(128)}, s32[]{}) while((s32[]{:T(128)}, u32[1024]{0:T(1024)S(1)}, u32[1024]{0:T(1024)S(1)}, s32[1024]{0:T(1024)S(1)}, s32[]{:T(128)}, /*index=5*/s32[]{:T(128)}, s32[]{}) %tuple.186), condition=%wide.region_2.3_spmd.clone, body=%wide.region_1.2_spmd.clone.sunk | while | flops 19460 | bytes 67685 | solution.py:110
  76.8 7.3 %all-to-all-start = ((f32[3,1,8,256]{3,1,0,2:T(1,128)}), f32[3,1,8,256]{3,1,0,2:T(1,128)S(1)}, u32[]{:S(2)}, u32[]{:S(2)}) async-start(f32[3,1,8,256]{3,1,0,2:T(1,128)} %copy.348), calls=%async_computation | async-start | bytes 49152 | tf_op jit(solution)/shard_map/all_to_all | solution.py:128
  93.0 26.6 %scatter_fusion = f32[2,4,2048]{1,0,2:T(2,128)S(1)} fusion(f32[2,4,2048]{1,0,2:T(2,128)S(1)} %broadcast.1405, s32[1024]{0:T(1024)S(1)} %broadcast_select_fusion, f32[1024,2,4]{2,1,0:T(2,128)S(1)} %copy.350), kind=kCustom, calls=%fused_computation.4 | custom fusion | bytes 102400
  121.5 6.0 all-to-all-start.1
  129.2 5.2 all-to-all-done.1
  134.4 30.9 %while.51 = (s32[]{:T(128)}, f32[4,8,64,64]{2,3,1,0:T(8,128)}, f32[4,8,64,2,4]{2,1,0,3,4:T(8,128)}, s32[4]{0:T(128)S(1)}, f32[3,1,1,8,256]{4,3,2,1,0:T(8,128)S(1...) while((s32[]{:T(128)}, f32[4,8,64,64]{2,3,1,0:T(8,128)}, ...), condition=%wide.region_7.8_spmd.clone.clone, body=%wide.region_6.7_spmd.clone.clone.sunk | while | flops 28427288 | bytes 1600791 | solution.py:76
  167.1 32.2 %all-reduce.2.cloned.1.call-done = f32[32,64,64]{1,2,0:T(8,128)} async-done(((f32[32,64,64]{1,2,0:T(8,128)}), f32[32,64,64]{1,2,0:T(8,128)}) %all-reduce.2.cloned.1.call-update) | async-done | bytes 524304 | tf_op jit(solution)/shard_map/psum | solution.py:131
  202.1 188.3 %custom-call.11 = f32[32,64,64]{2,1,0:T(8,128)} custom-call(f32[32,64,64]{2,1,0:T(8,128)S(1)} %fusion.24), custom_call_target="Cholesky" | custom-call | tf_op jit(solution)/shard_map/jit(cholesky)/cholesky | solution.py:85
  394.8 67.2 %custom-call.12 = f32[32,1,64,64]{0,2,3,1:T(8,128)S(1)} custom-call(f32[32,1,64,64]{0,3,2,1:T(8,128)} %select_bitcast_fusion), custom_call_target="InvertDiagBlocksLowerTriangular" | custom-call | tf_op jit(solution)/shard_map/jit(_solve_triangular)/vmap()/triangular_solve | solution.py:88
  473.8 5.9 all-to-all-start.2
  480.7 7.5 %all-to-all-done.2 = f32[8,1,8192]{2,1,0:T(1,128)S(1)} async-done(((f32[8,1,8192]{2,1,0:T(1,128)}), f32[8,1,8192]{2,1,0:T(1,128)S(1)}, u32[]{:S(2)}, u32[]{:S(2)}) %all-to-all-start.2) | async-done | bytes 262176 | tf_op jit(solution)/shard_map/all_to_all | solution.py:192
  496.5 4.9 copy.445
  501.4 7.3 %reshape.1555 = f32[8,1,16384]{2,1,0:T(1,128)} reshape(f32[512,1,2,2,8,8]{5,4,3,2,1,0:T(8,128)} %bitcast.594) | data formatting | bytes 1048576
  513.7 12.8 %all-to-all-done.3 = f32[8,1,16384]{2,1,0:T(1,128)S(1)} async-done(((f32[8,1,16384]{2,1,0:T(1,128)}), f32[8,1,16384]{2,1,0:T(1,128)S(1)}, u32[]{:S(2)}, u32[]{:S(2)}) %all-to-all-start.3) | async-done | bytes 524320 | tf_op jit(solution)/shard_map/all_to_all | solution.py:210
  528.4 7.8 %reshape.1556 = f32[512,1,2,2,8,8]{5,4,3,2,1,0:T(8,128)} reshape(f32[8,16384]{1,0:T(8,128)S(1)} %reduce.23) | data formatting | bytes 1048576
  536.2 5.4 copy.379
  548.8 12.5 %all_to_all.70 = f32[8,1,8192]{2,1,0:T(1,128)S(1)} all-to-all(f32[8,1,8192]{2,1,0:T(1,128)S(1)} %reshape.1557), channel_id=1, replica_groups=mesh['freq'=4,'lat'=8] {'lat'}, dimensions={0} | all-to-all | bytes 524288 | tf_op jit(solution)/shard_map/all_to_all | solution.py:192
  569.0 4.9 copy.448
  573.9 7.3 %reshape.1559 = f32[8,1,16384]{2,1,0:T(1,128)} reshape(f32[512,1,2,2,8,8]{5,4,3,2,1,0:T(8,128)} %bitcast.596) | data formatting | bytes 1048576
  585.8 13.1 %all-to-all-done.5 = f32[8,1,16384]{2,1,0:T(1,128)S(1)} async-done(((f32[8,1,16384]{2,1,0:T(1,128)}), f32[8,1,16384]{2,1,0:T(1,128)S(1)}, u32[]{:S(2)}, u32[]{:S(2)}) %all-to-all-start.5) | async-done | bytes 524320 | tf_op jit(solution)/shard_map/all_to_all | solution.py:210
  600.9 7.8 %reshape.1560 = f32[512,1,2,2,8,8]{5,4,3,2,1,0:T(8,128)} reshape(f32[8,16384]{1,0:T(8,128)S(1)} %reduce.25) | data formatting | bytes 1048576
  608.7 5.4 copy.394
  619.4 18.9 %reduce-scatter.8.cloned.1.call-done = f32[64,128]{1,0:T(8,128)} async-done(((f32[64,512]{1,0:T(8,128)}), f32[64,128]{1,0:T(8,128)}) %reduce-scatter.8.cloned.1.call-update) | async-done | bytes 32784 | tf_op jit(solution)/shard_map/reduce_scatter | solution.py:225
  (351 shorter events, 167.4 us)
Async XLA Ops:
  16.8 55.2 %copy-start.41 = (s32[2]{0:T(128)S(1)}, s32[2]{0:T(128)}, u32[]{:S(2)}) copy-start(s32[2]{0:T(128)} %constant.465) | copy-start | bytes 28
  16.9 55.3 %copy-start.40 = (s32[2]{0:T(128)S(1)}, s32[2]{0:T(128)}, u32[]{:S(2)}) copy-start(s32[2]{0:T(128)} %constant.468) | copy-start | bytes 28
  16.9 55.4 %copy-start.28 = (f32[2,1024]{1,0:T(2,128)S(1)}, f32[2,1024]{1,0:T(2,128)}, u32[]{:S(2)}) copy-start(f32[2,1024]{1,0:T(2,128)} %param.39) | copy-start | bytes 24580
  16.9 55.4 %copy-start.29 = (s32[1024]{0:T(1024)S(1)}, s32[1024]{0:T(1024)}, u32[]{:S(2)}) copy-start(s32[1024]{0:T(1024)} %param.38) | copy-start | bytes 12292
  16.9 55.4 %copy-start.30 = (f32[1024]{0:T(1024)S(1)}, f32[1024]{0:T(1024)}, u32[]{:S(2)}) copy-start(f32[1024]{0:T(1024)} %param.40) | copy-start | bytes 12292
  67.6 20.1 %copy-start.39 = (f32[2,8]{1,0:T(2,128)S(1)}, f32[2,8]{1,0:T(2,128)}, u32[]{:S(2)}) copy-start(f32[2,8]{1,0:T(2,128)} %param.42) | copy-start | bytes 196
  67.7 24.2 %copy-start.22 = (f32[2,4,1024]{2,1,0:T(4,128)S(1)}, f32[2,4,1024]{2,1,0:T(4,128)}, u32[]{:S(2)}) copy-start(f32[2,4,1024]{2,1,0:T(4,128)} %param.36) | copy-start | bytes 98308
  76.8 44.7 %all-to-all-start = ((f32[3,1,8,256]{3,1,0,2:T(1,128)}), f32[3,1,8,256]{3,1,0,2:T(1,128)S(1)}, u32[]{:S(2)}, u32[]{:S(2)}) async-start(f32[3,1,8,256]{3,1,0,2:T(1,128)} %copy.348), calls=%async_computation | async-start | bytes 49152 | tf_op jit(solution)/shard_map/all_to_all | solution.py:128
  121.5 12.9 %all-to-all-start.1 = ((f32[2,4,8,256]{3,1,0,2:T(4,128)}), f32[2,4,8,256]{3,1,0,2:T(4,128)S(1)}, u32[]{:S(2)}, u32[]{:S(2)}) async-start(f32[2,4,8,256]{3,1,0,2:T(4,128)} %copy.351), calls=%async_computation.1 | async-start | bytes 131072 | tf_op jit(solution)/shard_map/all_to_all | solution.py:127
  127.5 71.8 %all-reduce.2.cloned.1.call-start = ((), (), s32[]{:S(2)}) async-start(), calls=%async_computation.9 | async-start | bytes 2097152 | tf_op jit(solution)/shard_map/psum | solution.py:131
  134.4 31.2 %copy-start.13 = (f32[64,64]{1,0:T(8,128)S(1)}, f32[64,64]{1,0:T(8,128)}, u32[]{:S(2)}) copy-start(f32[64,64]{1,0:T(8,128)} %fusion.111) | copy-start | bytes 49156
  134.4 31.3 %copy-start.26 = (f32[1,8,2,8]{3,1,2,0:T(8,128)S(1)}, f32[1,8,2,8]{3,1,2,0:T(8,128)}, u32[]{:S(2)}) copy-start(f32[1,8,2,8]{3,1,2,0:T(8,128)} %get-tuple-element.409) | copy-start | bytes 1540
  134.4 31.4 %copy-start.25 = (f32[1,8,2,8]{3,1,2,0:T(8,128)S(1)}, f32[1,8,2,8]{3,1,2,0:T(8,128)}, u32[]{:S(2)}) copy-start(f32[1,8,2,8]{3,1,2,0:T(8,128)} %get-tuple-element.408) | copy-start | bytes 1540
  165.4 298.2 %reduce-scatter.4.cloned.1.call-start = ((), (), s32[]{:S(2)}) async-start(), calls=%async_computation.10 | async-start | bytes 163840 | tf_op jit(solution)/shard_map/reduce_scatter | solution.py:132
  165.7 33.6 %copy-start.5 = (f32[64,64]{0,1:T(8,128)}, f32[64,64]{0,1:T(8,128)S(1)}, u32[]{:S(2)}) copy-start(f32[64,64]{0,1:T(8,128)S(1)} %copy.355) | copy-start | bytes 49156
  473.8 14.4 %all-to-all-start.2 = ((f32[8,1,8192]{2,1,0:T(1,128)}), f32[8,1,8192]{2,1,0:T(1,128)S(1)}, u32[]{:S(2)}, u32[]{:S(2)}) async-start(f32[8,1,8192]{2,1,0:T(1,128)} %reshape.1553), calls=%async_computation.3 | async-start | bytes 524288 | tf_op jit(solution)/shard_map/all_to_all | solution.py:192
  479.9 15.6 %copy-start.9 = (f32[1,8,2,8]{1,3,0,2:T(8,128)}, f32[1,8,2,8]{1,3,0,2:T(8,128)S(1)}, u32[]{:S(2)}) copy-start(f32[1,8,2,8]{1,3,0,2:T(8,128)S(1)} %copy.342) | copy-start | bytes 1540
  479.9 15.5 %copy-start.11 = (f32[1,8,2,8]{1,3,0,2:T(8,128)}, f32[1,8,2,8]{1,3,0,2:T(8,128)S(1)}, u32[]{:S(2)}) copy-start(f32[1,8,2,8]{1,3,0,2:T(8,128)S(1)} %copy.343) | copy-start | bytes 1540
  480.0 11.9 %copy-start.17 = (f32[8,8]{1,0:T(8,128)}, f32[8,8]{1,0:T(8,128)S(1)}, u32[]{:S(2)}) copy-start(f32[8,8]{1,0:T(8,128)S(1)} %fusion.131) | copy-start | bytes 772
  508.8 17.7 %all-to-all-start.3 = ((f32[8,1,16384]{2,1,0:T(1,128)}), f32[8,1,16384]{2,1,0:T(1,128)S(1)}, u32[]{:S(2)}, u32[]{:S(2)}) async-start(f32[8,1,16384]{2,1,0:T(1,128)} %reshape.1555), calls=%async_computation.4 | async-start | bytes 1048576 | tf_op jit(solution)/shard_map/all_to_all | solution.py:210
  581.2 17.8 %all-to-all-start.5 = ((f32[8,1,16384]{2,1,0:T(1,128)}), f32[8,1,16384]{2,1,0:T(1,128)S(1)}, u32[]{:S(2)}, u32[]{:S(2)}) async-start(f32[8,1,16384]{2,1,0:T(1,128)} %reshape.1559), calls=%async_computation.6 | async-start | bytes 1048576 | tf_op jit(solution)/shard_map/all_to_all | solution.py:210
  584.8 34.6 %reduce-scatter.6.cloned.1.call-start = ((), (), s32[]{:S(2)}) async-start(), calls=%async_computation.11 | async-start | bytes 163840 | tf_op jit(solution)/shard_map/reduce_scatter | solution.py:225
  585.5 52.7 %reduce-scatter.8.cloned.1.call-start = ((), (), s32[]{:S(2)}) async-start(), calls=%async_computation.12 | async-start | bytes 163840 | tf_op jit(solution)/shard_map/reduce_scatter | solution.py:225
  618.6 21.0 %copy-start.2 = (f32[2,64,512]{2,1,0:T(8,128)}, f32[2,64,512]{2,1,0:T(8,128)S(1)}, u32[]{:S(2)}) copy-start(f32[2,64,512]{2,1,0:T(8,128)S(1)} %fusion.46) | copy-start | bytes 786436
  (27 other events, 117.4 us)
Sparse Core Ops, SparseCore 0:
  165.5 33.8 all-reduce.1
  202.3 20.4 reduce-scatter.3
  588.0 21.0 reduce-scatter.5
  619.5 18.7 reduce-scatter.7
where the time goes:
time: 656 us; the launch traced here: 647 us
  other arithmetic  302 us (46%)
  local copies, waits for them, and re-layouts  166 us (25%)
  waiting for transfers between devices  89.8 us (14%)
  matrix products  29.4 us (4%)
  starting transfers between devices  27.1 us (4%)
  between operations  16.1 us (2%)
  blocking collectives  12.5 us (2%)
    another operation x4, other arithmetic, fit_grid(): factor = jnp.linalg.cholesky(system)  190 us
    another operation x3, other arithmetic, fit_grid(): jax.scipy.linalg.solve_triangular(factor, middle, lower=True, trans='T')  69.5 us
    unnamed x96, local copies, waits for them, and re-layouts  63.4 us
    gather x11, local copies, waits for them, and re-layouts, local(): firsts = jnp.searchsorted(sorted_tiles, sorted_tiles, side='left')  49.8 us
    psum x1, waiting for transfers between devices, local(): normal = lax.psum(normal, 'freq')  32.2 us
    all_to_all x2, waiting for transfers between devices, local(): lax.all_to_all(columns, 'lat', split_axis=5, concat_axis=2, tiled=True)  25.9 us
    reduce_scatter x2, waiting for transfers between devices, local(): lax.psum_scatter(summed, 'freq', scatter_dimension=1, tiled=True)  18.9 us
  transfers between devices with their start and end apart: 9, of which 6 were waited for; matrix products, arithmetic and copies ran while one was open for 51% of the time, Pallas kernels for 0%

commit v1 on v0

v1 whole, which is shorter than its diff:
```python
import functools
import math

import jax
import jax.numpy as jnp
import numpy as np
from jax import lax
from jax.experimental import pallas as pl
from jax.experimental.pallas import tpu as pltpu
from jax.sharding import PartitionSpec as P

TB = 32
MODES = 8
CAP = 8
TERMS = MODES * MODES

damping = 1.0
depth_step = 1.0

NN = (((1,), (0,)), ((), ()))
NT = (((1,), (1,)), ((), ()))
VMEM = pl.BlockSpec(memory_space=pltpu.VMEM)


def dft_tables(length):
    at = np.arange(length)
    angle = 2.0 * math.pi / length * (at[:, None] * at[None, :] % length)
    exact = np.stack([np.cos(angle), np.sin(angle)], 0)
    high = exact.astype(jnp.bfloat16)
    low = (exact - high.astype(np.float64)).astype(jnp.bfloat16)
    return high, low


def mode_tables(length):
    at = np.arange(length)
    angle = 2.0 * math.pi / length * (at[:, None] * at[None, :] % length)
    cosines = np.cos(math.pi * np.arange(MODES)[:, None] * (np.arange(TB)[None, :] + 0.5) / TB)
    fold = np.zeros((length // TB, MODES, length))
    for tile in range(length // TB):
        fold[tile, :, tile * TB : (tile + 1) * TB] = cosines
    fold = fold.reshape(length // TB * MODES, length)
    return np.concatenate([fold @ np.cos(angle), -(fold @ np.sin(angle))], 1).astype(np.float32)


def split2(x):
    high = x.astype(jnp.bfloat16)
    return high, (x - high.astype(jnp.float32)).astype(jnp.bfloat16)


def dot3(a, b, dims=NN):
    one = functools.partial(lax.dot_general, dimension_numbers=dims, preferred_element_type=jnp.float32)
    return one(a[0], b[0]) + (one(a[0], b[1]) + one(a[1], b[0]))


def route_kernel(slot_ref, feat_ref, out_ref):
    feats = feat_ref[...]
    high = feats.astype(jnp.bfloat16)
    rest = feats - high.astype(jnp.float32)
    middle = rest.astype(jnp.bfloat16)
    low = (rest - middle.astype(jnp.float32)).astype(jnp.bfloat16)
    parts = jnp.concatenate([high, middle, low], 0)
    rows = feats.shape[0]
    slot = slot_ref[...]
    width = 256
    for at in range(0, out_ref.shape[1], width):
        places = lax.broadcasted_iota(jnp.int32, (width, slot.shape[1]), 0) + at
        chosen = jnp.where(places == slot, 1.0, 0.0).astype(jnp.bfloat16)
        got = lax.dot_general(parts, chosen, NT, preferred_element_type=jnp.float32)
        out_ref[:, at : at + width] = got[:rows] + got[rows : 2 * rows] + got[2 * rows :]


def fit_kernel(tiles, got_ref, out_ref, system):
    count = got_ref.shape[1]
    data_rows = got_ref.shape[0] - 3
    weight = got_ref[data_rows : data_rows + 1, :]

    def chebyshev(cosine):
        terms = [jnp.ones_like(cosine), cosine]
        for _ in range(MODES - 2):
            terms.append(2.0 * cosine * terms[-1] - terms[-2])
        return terms

    along_x = chebyshev(got_ref[data_rows + 1 : data_rows + 2, :])
    along_y = jnp.concatenate(chebyshev(got_ref[data_rows + 2 : data_rows + 3, :]), 0)
    basis = jnp.concatenate([term * along_y for term in along_x], 0)
    right = jnp.concatenate([basis, got_ref[:data_rows, :]], 0)
    weighted = basis * weight
    lane = lax.broadcasted_iota(jnp.int32, (1, count), 1)
    tile_of = lax.div(lax.rem(lane, tiles * CAP), CAP)
    width = TERMS + data_rows
    eye = jnp.where(
        lax.broadcasted_iota(jnp.int32, (TERMS, width), 0)
        == lax.broadcasted_iota(jnp.int32, (TERMS, width), 1),
        damping,
        0.0,
    )
    left = jnp.concatenate([jnp.where(tile_of == tile, weighted, 0.0) for tile in range(tiles)], 0)
    summed = lax.dot_general(
        left, right, NT, preferred_element_type=jnp.float32, precision=lax.Precision.HIGHEST
    )
    system[...] = summed.reshape(tiles, TERMS, width) + eye[None]
    for k in range(TERMS):
        row = system[:, k : k + 1, :]
        scaled = row * (1.0 / row[:, :, k : k + 1])
        whole = system[...]
        system[...] = whole - whole[:, :, k : k + 1] * scaled
        system[:, k : k + 1, :] = scaled
    out_ref[...] = system[:, :, TERMS:]


def bands(real, imag, out_ref):
    count = out_ref.shape[0]
    band = real.shape[1] // count
    for dst in range(count):
        part = slice(dst * band, (dst + 1) * band)
        out_ref[dst] = jnp.concatenate([real[:, part], imag[:, part]], 1)


def modes_y_kernel(coef_ref, table_ref, out_ref):
    rows = coef_ref.shape[0] // 2
    length = table_ref.shape[1] // 2
    made = lax.dot_general(
        coef_ref[...],
        table_ref[...],
        NN,
        preferred_element_type=jnp.float32,
        precision=lax.Precision.HIGHEST,
    )
    real = made[:rows, :length] - made[rows:, length:]
    imag = made[:rows, length:] + made[rows:, :length]
    bands(real, imag, out_ref)


def swapped(x):
    half = x.shape[1] // 2
    return jnp.concatenate([x[:, half:], x[:, :half]], 1)


def column_kernel(from_modes, high_ref, low_ref, table_ref, got_ref, even_ref, odd_ref, out_ref):
    lanes = got_ref.shape[2]
    got = got_ref[...].reshape(-1, lanes)
    sign = jnp.where(lax.broadcasted_iota(jnp.int32, (1, lanes), 1) < lanes // 2, -1.0, 1.0)
    cosine = (high_ref[0], low_ref[0])
    sine = (high_ref[1], low_ref[1])
    if from_modes:
        length = table_ref.shape[0] // 2
        both = lax.dot_general(
            table_ref[...],
            got,
            NN,
            preferred_element_type=jnp.float32,
            precision=lax.Precision.HIGHEST,
        )
        spectrum = both[:length] + sign * swapped(both[length:])
    else:
        parts = split2(got)
        spectrum = dot3(cosine, parts) - sign * swapped(dot3(sine, parts))
    turned = swapped(spectrum)
    refs = even_ref.shape[0]
    moved = jnp.concatenate(
        [spectrum * even_ref[g] + turned * odd_ref[g] for g in range(refs)], 1
    )
    parts = split2(moved)
    straight = dot3(cosine, parts)
    crossed = dot3(sine, parts)
    rows = out_ref.shape[2]
    for g in range(refs):
        part = slice(g * lanes, (g + 1) * lanes)
        back = straight[:, part] + sign * swapped(crossed[:, part])
        for dst in range(out_ref.shape[0]):
            out_ref[dst, g] = back[dst * rows : (dst + 1) * rows]


def row_kernel(last, high_ref, low_ref, got_ref, cos_ref, sin_ref, group_ref, *out_refs):
    wave_ref = out_refs[0]
    count, refs, rows, lanes = got_ref.shape
    half = lanes // 2
    cosine = (high_ref[0], low_ref[0])
    sine = (high_ref[1], low_ref[1])
    real = jnp.concatenate(
        [got_ref[src, :, :, :half].reshape(refs * rows, half) for src in range(count)], 1
    )
    imag = jnp.concatenate(
        [got_ref[src, :, :, half:].reshape(refs * rows, half) for src in range(count)], 1
    )
    parts = split2(jnp.concatenate([real, imag], 0))
    straight = dot3(parts, cosine)
    crossed = dot3(parts, sine)
    total = refs * rows
    real = straight[:total] - crossed[total:]
    imag = straight[total:] + crossed[:total]
    group = group_ref[...]
    chosen_real, chosen_imag = real[:rows], imag[:rows]
    for g in range(1, refs):
        part = slice(g * rows, (g + 1) * rows)
        chosen_real = jnp.where(group == g, real[part], chosen_real)
        chosen_imag = jnp.where(group == g, imag[part], chosen_imag)
    along, across = cos_ref[...], sin_ref[...]
    real = chosen_real * along - chosen_imag * across
    imag = chosen_real * across + chosen_imag * along
    wave_ref[0] = real
    if last:
        wave_ref[1] = imag
        return
    parts = split2(jnp.concatenate([real, imag], 0))
    straight = dot3(parts, cosine)
    crossed = dot3(parts, sine)
    bands(
        straight[:rows] + crossed[rows:],
        straight[rows:] - crossed[:rows],
        out_refs[1],
    )


def call(kernel, shapes, flops, *operands, scratch=()):
    single = not isinstance(shapes, (list, tuple))
    out_shape = jax.tree.map(
        lambda s: jax.ShapeDtypeStruct(s.shape, jnp.float32), shapes
    )
    return pl.pallas_call(
        kernel,
        out_shape=out_shape,
        in_specs=[VMEM] * len(operands),
        out_specs=VMEM if single else [VMEM] * len(shapes),
        scratch_shapes=list(scratch),
        cost_estimate=pl.CostEstimate(flops=flops, bytes_accessed=4 << 20, transcendentals=0),
        compiler_params=pltpu.CompilerParams(vmem_limit_bytes=48 << 20),
    )(*operands)


def shaped(*dims):
    return jax.ShapeDtypeStruct(dims, jnp.float32)


def local(spectra, tile_route, bin_in_tile, trace_offset, weights, frequency, slowness, vel_index):
    freq_count = lax.axis_size("freq")
    lat_count = lax.axis_size("lat")
    devices = freq_count * lat_count
    steps, row_count, ny = vel_index.shape
    nx = row_count * lat_count
    total_tiles = (nx // TB) * (ny // TB)
    tiles = total_tiles // devices
    slots = tiles * CAP
    trace_count = spectra.shape[2]
    data_rows = 2 * spectra.shape[1]
    features = data_rows + 3

    tile_id = tile_route[:, 0]
    order = jnp.arange(trace_count)
    rank = jnp.sum(
        ((tile_id[:, None] == tile_id[None, :]) & (order[:, None] < order[None, :])).astype(
            jnp.int32
        ),
        0,
    )
    slab_tiles = total_tiles // lat_count
    owner = (tile_id % slab_tiles) // tiles * lat_count + tile_id // slab_tiles
    slot = owner * slots + (tile_id % tiles) * CAP + rank
    cell_x = (bin_in_tile // TB).astype(jnp.float32) + trace_offset[0]
    cell_y = (bin_in_tile % TB).astype(jnp.float32) + trace_offset[1]
    padded_rows = -(-features // 16) * 16
    feats = jnp.concatenate(
        [
            spectra.reshape(data_rows, trace_count),
            weights[None],
            jnp.cos(math.pi * (cell_x[None] + 0.5) / TB),
            jnp.cos(math.pi * (cell_y[None] + 0.5) / TB),
            jnp.zeros((padded_rows - features, trace_count), jnp.float32),
        ],
        0,
    )
    placed = call(
        route_kernel, shaped(padded_rows, devices * slots), 1 << 28, slot[None], feats
    )
    sent = placed[:features].reshape(features, devices, slots).transpose(1, 0, 2)
    got = lax.all_to_all(sent, ("freq", "lat"), split_axis=0, concat_axis=0, tiled=True)
    got = got.transpose(1, 0, 2).reshape(features, devices * slots)
    coeffs = call(
        functools.partial(fit_kernel, tiles),
        shaped(tiles, TERMS, data_rows),
        1 << 30,
        got,
        scratch=[pltpu.VMEM((tiles, TERMS, TERMS + data_rows), jnp.float32)],
    )
    coeffs = coeffs.reshape(tiles, TERMS, 2, freq_count, -1).transpose(3, 0, 1, 2, 4)
    coeffs = lax.all_to_all(coeffs, "freq", split_axis=0, concat_axis=0, tiled=True)
    tile_rows = row_count // TB
    coeffs = coeffs.reshape(tile_rows, ny // TB, MODES, MODES, 2).transpose(4, 0, 2, 1, 3)
    mode_rows = tile_rows * MODES
    coeffs = coeffs.reshape(2 * mode_rows, ny // TB * MODES)

    high, low = dft_tables(nx)
    table = mode_tables(nx)
    high, low = jnp.asarray(high), jnp.asarray(low)
    table_y, table_x = jnp.asarray(table), jnp.asarray(np.ascontiguousarray(table.T))
    band = ny // lat_count
    refs = 2
    per_group = slowness.shape[1] // refs
    lat_at = lax.axis_index("lat")
    ky_index = lat_at * band + jnp.arange(2 * band) % band
    ky_vals = 2.0 * math.pi / ny * jnp.where(ky_index >= ny // 2, ky_index - ny, ky_index).astype(
        jnp.float32
    )
    kx_index = jnp.arange(nx)
    kx_vals = 2.0 * math.pi / nx * jnp.where(kx_index >= nx // 2, kx_index - nx, kx_index).astype(
        jnp.float32
    )
    odd_sign = jnp.where(jnp.arange(2 * band) < band, -1.0, 1.0)
    inverse_scale = 1.0 / (nx * ny)

    packed = call(
        modes_y_kernel, shaped(lat_count, mode_rows, 2 * band), 1 << 26, coeffs, table_y
    )
    images = []
    for depth_at in range(steps):
        table_row = slowness[depth_at]
        references = table_row.reshape(refs, per_group).mean(axis=1)
        wave_num = frequency[0] * references
        vertical = (
            (wave_num * wave_num)[:, None, None]
            - (kx_vals * kx_vals)[None, :, None]
            - (ky_vals * ky_vals)[None, None, :]
        )
        phase = jnp.sqrt(jnp.maximum(vertical, 0.0)) * depth_step
        damped = jnp.exp(-jnp.sqrt(jnp.maximum(-vertical, 0.0)) * depth_step)
        even = damped * jnp.cos(phase)
        odd = damped * jnp.sin(phase) * odd_sign
        velocity = vel_index[depth_at]
        picked = velocity[None] == jnp.arange(slowness.shape[1])[:, None, None]
        shift_of = (table_row.reshape(refs, per_group) - references[:, None]).reshape(-1)
        split_phase = (
            frequency[0]
            * jnp.sum(jnp.where(picked, shift_of[:, None, None], 0.0), 0)
            * depth_step
        )
        group = velocity // per_group
        along = jnp.cos(split_phase) * inverse_scale
        across = jnp.sin(split_phase) * inverse_scale

        columns = lax.all_to_all(packed, "lat", split_axis=0, concat_axis=0, tiled=True)
        moved = call(
            functools.partial(column_kernel, depth_at == 0),
            shaped(lat_count, refs, row_count, 2 * band),
            1 << 30,
            high,
            low,
            table_x,
            columns,
            even,
            odd,
        )
        rows = lax.all_to_all(moved, "lat", split_axis=0, concat_axis=0, tiled=True)
        last = depth_at == steps - 1
        shapes = [shaped(2 if last else 1, row_count, ny)]
        if not last:
            shapes.append(shaped(lat_count, row_count, 2 * band))
        made = call(
            functools.partial(row_kernel, last),
            shapes,
            1 << 30,
            high,
            low,
            rows,
            along,
            across,
            group,
        )
        wave_field = made[0]
        if not last:
            packed = made[1]
        split = wave_field[0].reshape(row_count, freq_count, ny // freq_count).transpose(1, 0, 2)
        images.append(split)
    split = lax.all_to_all(jnp.stack(images, 1), "freq", split_axis=0, concat_axis=0, tiled=True)
    return (wave_field[:, None], jnp.sum(split, 0))


def solution(mesh):
    return jax.shard_map(
        local,
        mesh=mesh,
        in_specs=(
            P(None, None, ("freq", "lat")),
            P(("freq", "lat"), None),
            P(("freq", "lat")),
            P(None, ("freq", "lat")),
            P(("freq", "lat")),
            P("freq"),
            P(),
            P(None, "lat", None),
        ),
        out_specs=(P(None, "freq", "lat", None), P(None, "lat", "freq")),
        check_vma=False,
    )
```

time: 656 us -> 129 us (0.20); the launches traced: 647 us -> 128 us
  other arithmetic: 302 us -> 13.3 us
  local copies, waits for them, and re-layouts: 166 us -> 10.5 us
  waiting for transfers between devices: 89.8 us -> 36.2 us
  matrix products: 29.4 us -> 0 us
  Pallas kernels: 0 us -> 22.7 us
  between operations: 16.1 us -> 1.53 us
  blocking collectives: 12.5 us -> 20.7 us
    another operation x26 -> x1, other arithmetic: 266 us -> 0.03 us  [local(): jnp.stack(images, 1)]
    unnamed x96 -> x28, local copies, waits for them, and re-layouts: 63.4 us -> 4.69 us
    gather x12 -> x0, local copies, waits for them, and re-layouts: 54.3 us -> none  [the longest x11 49.8 us: local(): firsts = jnp.searchsorted(sorted_tiles, sorted_tiles, side='left')]
    psum x1 -> x0, waiting for transfers between devices: 32.2 us -> none  [local(): normal = lax.psum(normal, 'freq')]
    dot_general x26 -> x0, matrix products: 25.9 us -> none  [the longest x4 5.52 us: one_block(): jnp.einsum('iabgc,jabgc->gij', weighted, basis_vals, precision=lax.Precis...]
    pallas_call x0 -> x7, Pallas kernels: none -> 22.7 us  [call(): pl.pallas_call(kernel, out_shape=out_shape, in_specs=[VMEM] * len(operand...]
    reduce_scatter x3 -> x0, waiting for transfers between devices: 18.9 us -> none  [the longest x2 18.9 us: local(): lax.psum_scatter(summed, 'freq', scatter_dimension=1, tiled=True)]
    all_to_all x4 -> x2, local copies, waits for them, and re-layouts: 12.1 us -> 0.52 us  [the longest x1 0.51 us: local(): lax.all_to_all(sent, ('freq', 'lat'), split_axis=0, concat_axis=0, tiled=...]
  transfers between devices with their start and end apart: 9 -> 5, of which waited for: 6 -> 5; matrix products, arithmetic and copies ran while one was open for 51% -> 7% of each run, Pallas kernels for 0% -> 0%
where the time goes in v1:
time: 129 us; the launch traced here: 128 us
  waiting for transfers between devices  36.2 us (28%)
  starting transfers between devices  23.4 us (18%)
  Pallas kernels  22.7 us (18%)
  blocking collectives  20.7 us (16%)
  other arithmetic  13.3 us (10%)
  local copies, waits for them, and re-layouts  10.5 us (8%)
  between operations  1.53 us (1%)
    all_to_all x2, waiting for transfers between devices, local(): rows = lax.all_to_all(moved, 'lat', split_axis=0, concat_axis=0, tiled=True)  25.6 us
    pallas_call x7, Pallas kernels, call(): pl.pallas_call(kernel, out_shape=out_shape, in_specs=[VMEM] * len(operand...  22.7 us
    all_to_all x1, blocking collectives, local(): lax.all_to_all(packed, 'lat', split_axis=0, concat_axis=0, tiled=True)  12.3 us
    all_to_all x2, starting transfers between devices, local(): rows = lax.all_to_all(moved, 'lat', split_axis=0, concat_axis=0, tiled=True)  9.13 us
    all_to_all x1, blocking collectives, local(): lax.all_to_all(jnp.stack(images, 1), 'freq', split_axis=0, concat_axis=0,...  8.39 us
    all_to_all x1, starting transfers between devices, local(): lax.all_to_all(sent, ('freq', 'lat'), split_axis=0, concat_axis=0, tiled=...  7.33 us
    all_to_all x1, waiting for transfers between devices, local(): lax.all_to_all(sent, ('freq', 'lat'), split_axis=0, concat_axis=0, tiled=...  6.4 us
    mul x1, other arithmetic, local(): odd = damped * jnp.sin(phase) * odd_sign  5.86 us
  transfers between devices with their start and end apart: 5, of which 5 were waited for; matrix products, arithmetic and copies ran while one was open for 7% of the time, Pallas kernels for 0%

profile of v1, /device:TPU:0, one launch (start us, length us, event | category | flops | bytes accessed | tf_op | source)
XLA Modules:
  0.0 128.3 jit_solution(2012407331916103123)
XLA Ops:
  2.2 1.2 convert_reduce_fusion
  5.6 1.3 %shard_map.131 = f32[16,2048]{1,0:T(8,128)S(1)} custom-call(s32[1,1024]{1,0:T(1,128)S(1)} %add_add_fusion.slot_ref, f32[16,1024]{1,0:T(8,128)S(1)} %concatenate.3.feat_ref), custom_call_target="tpu_custom_call" | custom-call | flops 268435456 | bytes 4194304 | tf_op jit(solution)/shard_map/pallas_call | solution.py:220
  7.9 7.3 %all-to-all-start = ((f32[32,1,704]{2,1,0:T(1,128)}), f32[32,1,704]{2,1,0:T(1,128)S(1)}, u32[]{:S(2)}, u32[]{:S(2)}) async-start(f32[32,1,704]{2,1,0:T(1,128)} %reshape.374), calls=%async_computation | async-start | bytes 196608 | tf_op jit(solution)/shard_map/all_to_all | solution.py:276
  16.5 6.4 %all-to-all-done = f32[32,1,704]{2,1,0:T(1,128)S(1)} async-done(((f32[32,1,704]{2,1,0:T(1,128)}), f32[32,1,704]{2,1,0:T(1,128)S(1)}, u32[]{:S(2)}, u32[]{:S(2)}) %all-to-all-start) | async-done | bytes 90144 | tf_op jit(solution)/shard_map/all_to_all | solution.py:276
  24.5 10.4 %shard_map.132 = f32[8,64,8]{2,1,0:T(8,128)S(1)} custom-call(f32[11,2048]{1,0:T(8,128)S(1)} %reshape.358.got_ref), custom_call_target="tpu_custom_call" | custom-call | flops 1073741824 | bytes 4194304 | tf_op jit(solution)/shard_map/pallas_call | solution.py:220
  35.7 3.4 %all-to-all-start.1 = ((f32[4,1,1024]{2,1,0:T(1,128)}), f32[4,1,1024]{2,1,0:T(1,128)S(1)}, u32[]{:S(2)}, u32[]{:S(2)}) async-start(f32[4,1,1024]{2,1,0:T(1,128)} %reshape.376), calls=%async_computation.1 | async-start | bytes 32768 | tf_op jit(solution)/shard_map/all_to_all | solution.py:286
  39.2 3.6 %all-to-all-done.1 = f32[4,1,1024]{2,1,0:T(1,128)S(1)} async-done(((f32[4,1,1024]{2,1,0:T(1,128)}), f32[4,1,1024]{2,1,0:T(1,128)S(1)}, u32[]{:S(2)}, u32[]{:S(2)}) %all-to-all-start.1) | async-done | bytes 16416 | tf_op jit(solution)/shard_map/all_to_all | solution.py:286
  44.0 1.1 shard_map.133
  45.0 3.5 %all-to-all-start.2 = ((f32[8,16,128]{2,1,0:T(8,128)}), f32[8,16,128]{2,1,0:T(8,128)S(1)}, u32[]{:S(2)}, u32[]{:S(2)}) async-start(f32[8,16,128]{2,1,0:T(8,128)} %shard_map.133), calls=%async_computation.2 | async-start | bytes 131072 | tf_op jit(solution)/shard_map/all_to_all | solution.py:340
  48.6 5.9 %fusion.17 = (f32[2,512,128]{2,1,0:T(8,128)S(1)}, f32[2,512,128]{2,1,0:T(8,128)}, f32[2,512,128]{2,1,0:T(8,128)}, f32[2,512,128]{2,1,0:T(8,128)}) fusion(f32[2,512]{1,0:T(2,128)S(1)} %get-tuple-element.32, f32[128]{0:T(128)S(1)} %get-tuple-element.44, f32[128]{0:T(128)S(1)} %get-tuple-element.45, f32[2,512]{1,0:T(2,128)S(1)} %get-tuple-element.33), kind=kLoop, calls=%fused_computation.27 | loop fusion | flops 2097152 | bytes 2106368 | tf_op jit(solution)/shard_map/mul | solution.py:327
  55.4 1.0 copy-done.5
  56.4 1.0 copy-done.6
  57.5 2.5 %shard_map.134 = f32[8,2,64,128]{3,2,1,0:T(8,128)} custom-call(bf16[2,512,512]{2,1,0:T(8,128)(2,1)S(1)} %copy-done, bf16[2,512,512]{2,1,0:T(8,128)(2,1)S(1)} %copy-done.1, f32[1024,128]{1,0:T(8,128)S(1)} %copy-done.2, f32[8,16,128]{2,1,0:T(8,128)S(1)} %all-to-all-done.2.got_ref, f32[2,512,128]{2,1,0:T(8,128)S(1)} %copy-done.5, f32[2,512,128]{2,1,0:T(8,128)S(1)} %copy-done.6), custom_call_target="tpu_custom_call" | custom-call | flops 1073741824 | bytes 4194304 | tf_op jit(solution)/shard_map/pallas_call | solution.py:220
  60.0 5.4 %all-to-all-start.3 = ((f32[8,2,64,128]{3,2,1,0:T(8,128)}), f32[8,2,64,128]{3,2,1,0:T(8,128)}, u32[]{:S(2)}, u32[]{:S(2)}) async-start(f32[8,2,64,128]{3,2,1,0:T(8,128)} %shard_map.134), calls=%async_computation.3 | async-start | bytes 1048576 | tf_op jit(solution)/shard_map/all_to_all | solution.py:352
  67.6 12.1 %all-to-all-done.3.got_ref = f32[8,2,64,128]{3,2,1,0:T(8,128)} async-done(((f32[8,2,64,128]{3,2,1,0:T(8,128)}), f32[8,2,64,128]{3,2,1,0:T(8,128)}, u32[]{:S(2)}, u32[]{:S(2)}) %all-to-all-start.3) | async-done | bytes 524320 | tf_op jit(solution)/shard_map/all_to_all | solution.py:352
  79.7 0.9 copy-done.8
  80.6 2.8 %shard_map.135 = (f32[1,64,512]{2,1,0:T(8,128)S(1)}, f32[8,64,128]{2,1,0:T(8,128)S(1)}) custom-call(bf16[2,512,512]{2,1,0:T(8,128)(2,1)S(1)} %copy-done, bf16[2,512,512]{2,1,0:T(8,128)(2,1)S(1)} %copy-done.1, f32[8,2,64,128]{3,2,1,0:T(8,128)} %all-to-all-done.3.got_ref, f32[64,512]{1,0:T(8,128)S(1)} %get-tuple-element.23.cos_ref, ...), custom_call_target="tpu_custom_call" | custom-call | flops 1073741824 | bytes 4194304 | tf_op jit(solution)/shard_map/pallas_call | solution.py:220
  83.4 12.3 %all_to_all.35.got_ref = f32[8,64,128]{2,1,0:T(8,128)S(1)} all-to-all(f32[8,64,128]{2,1,0:T(8,128)S(1)} %get-tuple-element.4), channel_id=1, replica_groups=mesh['freq'=4,'lat'=8] {'lat'}, dimensions={0} | all-to-all | bytes 524288 | tf_op jit(solution)/shard_map/all_to_all | solution.py:340
  95.7 2.8 %shard_map.136 = f32[8,2,64,128]{3,2,1,0:T(8,128)} custom-call(bf16[2,512,512]{2,1,0:T(8,128)(2,1)S(1)} %copy-done, bf16[2,512,512]{2,1,0:T(8,128)(2,1)S(1)} %copy-done.1, f32[1024,128]{1,0:T(8,128)S(1)} %copy-done.2, f32[8,64,128]{2,1,0:T(8,128)S(1)} %all_to_all.35.got_ref, f32[2,512,128]{2,1,0:T(8,128)S(1)} %copy-done.3, ...), custom_call_target="tpu_custom_call" | custom-call | flops 1073741824 | bytes 4194304 | tf_op jit(solution)/shard_map/pallas_call | solution.py:220
  98.5 3.7 %all-to-all-start.5 = ((f32[8,2,64,128]{3,2,1,0:T(8,128)}), f32[8,2,64,128]{3,2,1,0:T(8,128)S(1)}, u32[]{:S(2)}, u32[]{:S(2)}) async-start(f32[8,2,64,128]{3,2,1,0:T(8,128)} %shard_map.136), calls=%async_computation.5 | async-start | bytes 1048576 | tf_op jit(solution)/shard_map/all_to_all | solution.py:352
  103.0 13.4 %all-to-all-done.5.got_ref = f32[8,2,64,128]{3,2,1,0:T(8,128)S(1)} async-done(((f32[8,2,64,128]{3,2,1,0:T(8,128)}), f32[8,2,64,128]{3,2,1,0:T(8,128)S(1)}, u32[]{:S(2)}, u32[]{:S(2)}) %all-to-all-start.5) | async-done | bytes 524320 | tf_op jit(solution)/shard_map/all_to_all | solution.py:352
  116.4 1.8 %shard_map.137 = f32[2,64,512]{2,1,0:T(8,128)} custom-call(bf16[2,512,512]{2,1,0:T(8,128)(2,1)S(1)} %copy-done, bf16[2,512,512]{2,1,0:T(8,128)(2,1)S(1)} %copy-done.1, f32[8,2,64,128]{3,2,1,0:T(8,128)S(1)} %all-to-all-done.5.got_ref, f32[64,512]{1,0:T(8,128)S(1)} %get-tuple-element.21.cos_ref, f32[64,512]{1,0:T(8,128)S(1)} %get-tuple-element.20.sin_ref, ...), custom_call_target="tpu_custom_call" | custom-call | flops 1073741824 | bytes 4194304 | tf_op jit(solution)/shard_map/pallas_call | solution.py:220
  118.2 0.9 slice.33
  119.2 8.4 %all_to_all.36 = f32[4,2,64,128]{3,2,1,0:T(8,128)S(1)} all-to-all(f32[4,2,64,128]{3,2,1,0:T(8,128)S(1)} %pad_maximum_fusion), channel_id=1, replica_groups=mesh['freq'=4,'lat'=8] {'freq'}, dimensions={0} | all-to-all | bytes 524288 | tf_op jit(solution)/shard_map/all_to_all | solution.py:373
  (71 shorter events, 13.5 us)
Async XLA Ops:
  5.6 10.3 %copy-start.11 = (f32[2,8]{1,0:T(2,128)S(1)}, f32[2,8]{1,0:T(2,128)}, u32[]{:S(2)}) copy-start(f32[2,8]{1,0:T(2,128)} %param.18) | copy-start | bytes 196
  7.9 14.9 %all-to-all-start = ((f32[32,1,704]{2,1,0:T(1,128)}), f32[32,1,704]{2,1,0:T(1,128)S(1)}, u32[]{:S(2)}, u32[]{:S(2)}) async-start(f32[32,1,704]{2,1,0:T(1,128)} %reshape.374), calls=%async_computation | async-start | bytes 196608 | tf_op jit(solution)/shard_map/all_to_all | solution.py:276
  34.9 9.1 %copy-start.4 = (f32[128,1024]{1,0:T(8,128)S(1)}, f32[128,1024]{1,0:T(8,128)}, u32[]{:S(2)}) copy-start(f32[128,1024]{1,0:T(8,128)} %constant.146.clone.table_ref) | copy-start | bytes 1572868
  35.7 7.1 %all-to-all-start.1 = ((f32[4,1,1024]{2,1,0:T(1,128)}), f32[4,1,1024]{2,1,0:T(1,128)S(1)}, u32[]{:S(2)}, u32[]{:S(2)}) async-start(f32[4,1,1024]{2,1,0:T(1,128)} %reshape.376), calls=%async_computation.1 | async-start | bytes 32768 | tf_op jit(solution)/shard_map/all_to_all | solution.py:286
  45.0 10.3 %copy-start.2 = (f32[1024,128]{1,0:T(8,128)S(1)}, f32[1024,128]{1,0:T(8,128)}, u32[]{:S(2)}) copy-start(f32[1024,128]{1,0:T(8,128)} %constant.147.clone.table_ref) | copy-start | bytes 1572868
  45.0 10.3 %all-to-all-start.2 = ((f32[8,16,128]{2,1,0:T(8,128)}), f32[8,16,128]{2,1,0:T(8,128)S(1)}, u32[]{:S(2)}, u32[]{:S(2)}) async-start(f32[8,16,128]{2,1,0:T(8,128)} %shard_map.133), calls=%async_computation.2 | async-start | bytes 131072 | tf_op jit(solution)/shard_map/all_to_all | solution.py:340
  48.5 6.8 %copy-start = (bf16[2,512,512]{2,1,0:T(8,128)(2,1)S(1)}, bf16[2,512,512]{2,1,0:T(8,128)(2,1)}, u32[]{:S(2)}) copy-start(bf16[2,512,512]{2,1,0:T(8,128)(2,1)} %constant.144.clone.high_ref) | copy-start | bytes 3145732
  48.5 6.8 %copy-start.1 = (bf16[2,512,512]{2,1,0:T(8,128)(2,1)S(1)}, bf16[2,512,512]{2,1,0:T(8,128)(2,1)}, u32[]{:S(2)}) copy-start(bf16[2,512,512]{2,1,0:T(8,128)(2,1)} %constant.145.clone.low_ref) | copy-start | bytes 3145732
  55.4 1.0 copy-start.5
  56.4 1.0 copy-start.6
  60.0 5.4 %copy-start.9 = (s32[2,64,512]{2,1,0:T(8,128)S(1)}, s32[2,64,512]{2,1,0:T(8,128)}, u32[]{:S(2)}) copy-start(s32[2,64,512]{2,1,0:T(8,128)} %param.19) | copy-start | bytes 786436
  60.0 19.7 %all-to-all-start.3 = ((f32[8,2,64,128]{3,2,1,0:T(8,128)}), f32[8,2,64,128]{3,2,1,0:T(8,128)}, u32[]{:S(2)}, u32[]{:S(2)}) async-start(f32[8,2,64,128]{3,2,1,0:T(8,128)} %shard_map.134), calls=%async_computation.3 | async-start | bytes 1048576 | tf_op jit(solution)/shard_map/all_to_all | solution.py:352
  79.7 0.9 copy-start.8
  80.6 15.1 %copy-start.3 = (f32[2,512,128]{2,1,0:T(8,128)S(1)}, f32[2,512,128]{2,1,0:T(8,128)}, u32[]{:S(2)}) copy-start(f32[2,512,128]{2,1,0:T(8,128)} %get-tuple-element.27.even_ref) | copy-start | bytes 1572868
  98.5 3.7 %copy-start.10 = (s32[64,512]{1,0:T(8,128)S(1)}, s32[64,512]{1,0:T(8,128)}, u32[]{:S(2)}) copy-start(s32[64,512]{1,0:T(8,128)} %get-tuple-element.18) | copy-start | bytes 393220
  98.5 17.9 %copy-start.7 = (s32[64,512]{1,0:T(8,128)S(1)}, s32[64,512]{1,0:T(8,128)}, u32[]{:S(2)}) copy-start(s32[64,512]{1,0:T(8,128)} %get-tuple-element.16.group_ref) | copy-start | bytes 393220
  98.5 17.9 %all-to-all-start.5 = ((f32[8,2,64,128]{3,2,1,0:T(8,128)}), f32[8,2,64,128]{3,2,1,0:T(8,128)S(1)}, u32[]{:S(2)}, u32[]{:S(2)}) async-start(f32[8,2,64,128]{3,2,1,0:T(8,128)} %shard_map.136), calls=%async_computation.5 | async-start | bytes 1048576 | tf_op jit(solution)/shard_map/all_to_all | solution.py:352

commit v2 on v1

--- a/solution.py
+++ b/solution.py
@@ -228,6 +228,53 @@
     )(*operands)
 
 
+def exchange_kernel(count, in_ref, out_ref, sent, landed, kept):
+    me = lax.axis_index("lat")
+    barrier = pltpu.get_barrier_semaphore()
+    partners = [lax.rem(me + step, count) for step in range(1, count)]
+    for partner in partners:
+        pl.semaphore_signal(
+            barrier, inc=1, device_id={"lat": partner}, device_id_type=pl.DeviceIdType.MESH
+        )
+    pl.semaphore_wait(barrier, count - 1)
+    copies = [
+        pltpu.make_async_remote_copy(
+            src_ref=in_ref.at[partner],
+            dst_ref=out_ref.at[me],
+            send_sem=sent.at[at],
+            recv_sem=landed.at[at],
+            device_id={"lat": partner},
+            device_id_type=pl.DeviceIdType.MESH,
+        )
+        for at, partner in enumerate(partners)
+    ]
+    for copy in copies:
+        copy.start()
+    own = pltpu.make_async_copy(in_ref.at[me], out_ref.at[me], kept)
+    own.start()
+    own.wait()
+    for copy in copies:
+        copy.wait()
+
+
+def exchange(blocks, number):
+    count = blocks.shape[0]
+    return pl.pallas_call(
+        functools.partial(exchange_kernel, count),
+        out_shape=jax.ShapeDtypeStruct(blocks.shape, blocks.dtype),
+        in_specs=[pl.BlockSpec(memory_space=pl.ANY)],
+        out_specs=pl.BlockSpec(memory_space=pl.ANY),
+        scratch_shapes=[
+            pltpu.SemaphoreType.DMA((count - 1,)),
+            pltpu.SemaphoreType.DMA((count - 1,)),
+            pltpu.SemaphoreType.DMA,
+        ],
+        compiler_params=pltpu.CompilerParams(
+            collective_id=number, has_side_effects=True, vmem_limit_bytes=1 << 20
+        ),
+    )(blocks)
+
+
 def shaped(*dims):
     return jax.ShapeDtypeStruct(dims, jnp.float32)
 
@@ -337,7 +384,10 @@
         along = jnp.cos(split_phase) * inverse_scale
         across = jnp.sin(split_phase) * inverse_scale
 
-        columns = lax.all_to_all(packed, "lat", split_axis=0, concat_axis=0, tiled=True)
+        if depth_at == 0:
+            columns = lax.all_to_all(packed, "lat", split_axis=0, concat_axis=0, tiled=True)
+        else:
+            columns = exchange(packed, 2 * depth_at)
         moved = call(
             functools.partial(column_kernel, depth_at == 0),
             shaped(lat_count, refs, row_count, 2 * band),
@@ -349,7 +399,7 @@
             even,
             odd,
         )
-        rows = lax.all_to_all(moved, "lat", split_axis=0, concat_axis=0, tiled=True)
+        rows = exchange(moved, 2 * depth_at + 1)
         last = depth_at == steps - 1
         shapes = [shaped(2 if last else 1, row_count, ny)]
         if not last:

time: 129 us -> 117 us (0.907)
  Pallas kernels: 22.7 us -> 52.3 us
  waiting for transfers between devices: 36.2 us -> 7.81 us
  blocking collectives: 20.7 us -> 8.39 us
  starting transfers between devices: 23.4 us -> 16.4 us
  local copies, waits for them, and re-layouts: 10.5 us -> 13.3 us
  other arithmetic: 13.3 us -> 15.5 us
    pallas_call x0 -> x3, Pallas kernels: none -> 32.3 us  [exchange(): pl.pallas_call(functools.partial(exchange_kernel, count), out_shape=jax.S...]
    all_to_all x2 -> x0, waiting for transfers between devices: 25.6 us -> none  [local(): rows = lax.all_to_all(moved, 'lat', split_axis=0, concat_axis=0, tiled=True)]
    all_to_all x1 -> x0, blocking collectives: 12.3 us -> none  [local(): lax.all_to_all(packed, 'lat', split_axis=0, concat_axis=0, tiled=True)]
    all_to_all x2 -> x0, starting transfers between devices: 9.13 us -> none  [local(): rows = lax.all_to_all(moved, 'lat', split_axis=0, concat_axis=0, tiled=True)]
    all_to_all x1, waiting for transfers between devices: 6.4 us -> 0.01 us  [local(): lax.all_to_all(sent, ('freq', 'lat'), split_axis=0, concat_axis=0, tiled=...]
    all_to_all x1, waiting for transfers between devices: 0.64 us -> 4.82 us  [local(): lax.all_to_all(packed, 'lat', split_axis=0, concat_axis=0, tiled=True)]
    pallas_call x7, Pallas kernels: 22.7 us -> 20 us  [call(): pl.pallas_call(kernel, out_shape=out_shape, in_specs=[VMEM] * len(operand...]
    all_to_all x1, starting transfers between devices: 3.48 us -> 5.81 us  [local(): lax.all_to_all(packed, 'lat', split_axis=0, concat_axis=0, tiled=True)]
  transfers between devices with their start and end apart: 5 -> 3, of which waited for: 5 -> 2; matrix products, arithmetic and copies ran while one was open for 7% -> 10% of each run, Pallas kernels for 0% -> 0%
where the time goes in v2:
time: 117 us; the launch traced here: 115 us
  Pallas kernels  52.3 us (45%)
  starting transfers between devices  16.4 us (14%)
  other arithmetic  15.5 us (13%)
  local copies, waits for them, and re-layouts  13.3 us (11%)
  blocking collectives  8.39 us (7%)
  waiting for transfers between devices  7.81 us (7%)
  between operations  1.66 us (1%)
    pallas_call x3, Pallas kernels, exchange(): pl.pallas_call(functools.partial(exchange_kernel, count), out_shape=jax.S...  32.3 us
    pallas_call x7, Pallas kernels, call(): pl.pallas_call(kernel, out_shape=out_shape, in_specs=[VMEM] * len(operand...  20 us
    all_to_all x1, blocking collectives, local(): lax.all_to_all(jnp.stack(images, 1), 'freq', split_axis=0, concat_axis=0,...  8.39 us
    all_to_all x1, starting transfers between devices, local(): lax.all_to_all(sent, ('freq', 'lat'), split_axis=0, concat_axis=0, tiled=...  7.33 us
    mul x1, other arithmetic, local(): odd = damped * jnp.sin(phase) * odd_sign  5.86 us
    all_to_all x1, starting transfers between devices, local(): lax.all_to_all(packed, 'lat', split_axis=0, concat_axis=0, tiled=True)  5.81 us
    unnamed x34, local copies, waits for them, and re-layouts  4.84 us
    all_to_all x1, waiting for transfers between devices, local(): lax.all_to_all(packed, 'lat', split_axis=0, concat_axis=0, tiled=True)  4.82 us
  transfers between devices with their start and end apart: 3, of which 2 were waited for; matrix products, arithmetic and copies ran while one was open for 10% of the time, Pallas kernels for 0%

profile of v2, /device:TPU:0, one launch (start us, length us, event | category | flops | bytes accessed | tf_op | source)
XLA Modules:
  0.0 115.4 jit_solution(5555091469970178287)
XLA Ops:
  2.2 1.2 %convert_reduce_fusion = s32[1024]{0:T(1024)S(1)} fusion(s32[1024]{0:T(1024)} %bitcast.87), kind=kLoop, calls=%fused_computation | loop fusion | flops 5241856 | bytes 8192 | tf_op jit(solution)/shard_map/reduce_sum | solution.py:297
  5.6 1.3 %shard_map.131 = f32[16,2048]{1,0:T(8,128)S(1)} custom-call(s32[1,1024]{1,0:T(1,128)S(1)} %add_add_fusion.slot_ref, f32[16,1024]{1,0:T(8,128)S(1)} %concatenate.3.feat_ref), custom_call_target="tpu_custom_call" | custom-call | flops 268435456 | bytes 4194304 | tf_op jit(solution)/shard_map/pallas_call | solution.py:220
  8.0 7.3 %all-to-all-start = ((f32[32,1,704]{2,1,0:T(1,128)}), f32[32,1,704]{2,1,0:T(1,128)S(1)}, u32[]{:S(2)}, u32[]{:S(2)}) async-start(f32[32,1,704]{2,1,0:T(1,128)} %reshape.374), calls=%async_computation | async-start | bytes 196608 | tf_op jit(solution)/shard_map/all_to_all | solution.py:323
  17.9 5.9 %fusion.17 = (f32[2,512,128]{2,1,0:T(8,128)S(1)}, f32[2,512,128]{2,1,0:T(8,128)}, f32[2,512,128]{2,1,0:T(8,128)}, f32[2,512,128]{2,1,0:T(8,128)}) fusion(f32[2,512]{1,0:T(2,128)S(1)} %get-tuple-element.32, f32[128]{0:T(128)S(1)} %get-tuple-element.44, f32[128]{0:T(128)S(1)} %get-tuple-element.45, f32[2,512]{1,0:T(2,128)S(1)} %get-tuple-element.33), kind=kLoop, calls=%fused_computation.27 | loop fusion | flops 2097152 | bytes 2106368 | tf_op jit(solution)/shard_map/mul | solution.py:374
  25.9 10.4 %shard_map.132 = f32[8,64,8]{2,1,0:T(8,128)S(1)} custom-call(f32[11,2048]{1,0:T(8,128)S(1)} %reshape.358.got_ref), custom_call_target="tpu_custom_call" | custom-call | flops 1073741824 | bytes 4194304 | tf_op jit(solution)/shard_map/pallas_call | solution.py:220
  37.1 3.3 %all-to-all-start.1 = ((f32[4,1,1024]{2,1,0:T(1,128)}), f32[4,1,1024]{2,1,0:T(1,128)S(1)}, u32[]{:S(2)}, u32[]{:S(2)}) async-start(f32[4,1,1024]{2,1,0:T(1,128)} %reshape.376), calls=%async_computation.1 | async-start | bytes 32768 | tf_op jit(solution)/shard_map/all_to_all | solution.py:333
  41.2 3.0 %all-to-all-done.1 = f32[4,1,1024]{2,1,0:T(1,128)S(1)} async-done(((f32[4,1,1024]{2,1,0:T(1,128)}), f32[4,1,1024]{2,1,0:T(1,128)S(1)}, u32[]{:S(2)}, u32[]{:S(2)}) %all-to-all-start.1) | async-done | bytes 16416 | tf_op jit(solution)/shard_map/all_to_all | solution.py:333
  45.8 1.7 %copy.32 = f32[2,2,8,16,8]{4,3,2,1,0:T(8,128)} copy(f32[2,2,8,16,8]{4,2,3,1,0:T(8,128)} %bitcast.76) | data formatting | bytes 32768 | tf_op jit(solution)/shard_map/transpose | solution.py:335
  47.5 1.1 reshape.361.coef_ref
  48.6 1.0 copy-done.4
  49.6 1.1 shard_map.133
  50.7 5.8 %all-to-all-start.2 = ((f32[8,16,128]{2,1,0:T(8,128)}), f32[8,16,128]{2,1,0:T(8,128)S(1)}, u32[]{:S(2)}, u32[]{:S(2)}) async-start(f32[8,16,128]{2,1,0:T(8,128)} %shard_map.133), calls=%async_computation.2 | async-start | bytes 131072 | tf_op jit(solution)/shard_map/all_to_all | solution.py:388
  56.5 2.1 %sine_multiply_fusion = (f32[64,512]{1,0:T(8,128)}, f32[64,512]{1,0:T(8,128)}) fusion(f32[64,512]{1,0:T(8,128)} %select_reduce_fusion, f32[]{:T(128)} %bitcast.71), kind=kLoop, calls=%fused_computation.46 | loop fusion | flops 98304 | bytes 393220 | tf_op jit(solution)/shard_map/mul | solution.py:385
  58.6 4.8 %all-to-all-done.2.got_ref = f32[8,16,128]{2,1,0:T(8,128)S(1)} async-done(((f32[8,16,128]{2,1,0:T(8,128)}), f32[8,16,128]{2,1,0:T(8,128)S(1)}, u32[]{:S(2)}, u32[]{:S(2)}) %all-to-all-start.2) | async-done | bytes 65568 | tf_op jit(solution)/shard_map/all_to_all | solution.py:388
  63.4 1.0 copy-done.5
  64.5 1.0 copy-done.6
  65.5 1.7 %shard_map.134.in_ref = f32[8,2,64,128]{3,2,1,0:T(8,128)S(1)} custom-call(bf16[2,512,512]{2,1,0:T(8,128)(2,1)S(1)} %copy-done, bf16[2,512,512]{2,1,0:T(8,128)(2,1)S(1)} %copy-done.1, f32[1024,128]{1,0:T(8,128)S(1)} %copy-done.2, f32[8,16,128]{2,1,0:T(8,128)S(1)} %all-to-all-done.2.got_ref, f32[2,512,128]{2,1,0:T(8,128)S(1)} %copy-done.5, ...), custom_call_target="tpu_custom_call" | custom-call | flops 1073741824 | bytes 4194304 | tf_op jit(solution)/shard_map/pallas_call | solution.py:220
  67.2 11.1 %shard_map.135.got_ref = f32[8,2,64,128]{3,2,1,0:T(8,128)S(1)} custom-call(f32[8,2,64,128]{3,2,1,0:T(8,128)S(1)} %shard_map.134.in_ref), custom_call_target="tpu_custom_call" | custom-call | tf_op jit(solution)/shard_map/pallas_call | solution.py:262
  78.3 1.7 %shard_map.136 = (f32[1,64,512]{2,1,0:T(8,128)S(1)}, f32[8,64,128]{2,1,0:T(8,128)S(1)}) custom-call(bf16[2,512,512]{2,1,0:T(8,128)(2,1)S(1)} %copy-done, bf16[2,512,512]{2,1,0:T(8,128)(2,1)S(1)} %copy-done.1, f32[8,2,64,128]{3,2,1,0:T(8,128)S(1)} %shard_map.135.got_ref, f32[64,512]{1,0:T(8,128)S(1)} %get-tuple-element.23.cos_ref, ...), custom_call_target="tpu_custom_call" | custom-call | flops 1073741824 | bytes 4194304 | tf_op jit(solution)/shard_map/pallas_call | solution.py:220
  80.1 8.6 %shard_map.137.got_ref = f32[8,64,128]{2,1,0:T(8,128)S(1)} custom-call(f32[8,64,128]{2,1,0:T(8,128)S(1)} %get-tuple-element.4.in_ref), custom_call_target="tpu_custom_call" | custom-call | tf_op jit(solution)/shard_map/pallas_call | solution.py:262
  88.7 2.1 %shard_map.138.in_ref = f32[8,2,64,128]{3,2,1,0:T(8,128)S(1)} custom-call(bf16[2,512,512]{2,1,0:T(8,128)(2,1)S(1)} %copy-done, bf16[2,512,512]{2,1,0:T(8,128)(2,1)S(1)} %copy-done.1, f32[1024,128]{1,0:T(8,128)S(1)} %copy-done.2, f32[8,64,128]{2,1,0:T(8,128)S(1)} %shard_map.137.got_ref, f32[2,512,128]{2,1,0:T(8,128)S(1)} %copy-done.3, ...), custom_call_target="tpu_custom_call" | custom-call | flops 1073741824 | bytes 4194304 | tf_op jit(solution)/shard_map/pallas_call | solution.py:220
  90.8 12.6 %shard_map.139.got_ref = f32[8,2,64,128]{3,2,1,0:T(8,128)S(1)} custom-call(f32[8,2,64,128]{3,2,1,0:T(8,128)S(1)} %shard_map.138.in_ref), custom_call_target="tpu_custom_call" | custom-call | tf_op jit(solution)/shard_map/pallas_call | solution.py:262
  103.5 1.8 %shard_map.140 = f32[2,64,512]{2,1,0:T(8,128)} custom-call(bf16[2,512,512]{2,1,0:T(8,128)(2,1)S(1)} %copy-done, bf16[2,512,512]{2,1,0:T(8,128)(2,1)S(1)} %copy-done.1, f32[8,2,64,128]{3,2,1,0:T(8,128)S(1)} %shard_map.139.got_ref, f32[64,512]{1,0:T(8,128)S(1)} %copy-done.8, f32[64,512]{1,0:T(8,128)S(1)} %copy-done.7, s32[64,512]{1,0:T(8,128)S(1)} %copy-done.11), custom_call_target="tpu_custom_call" | custom-call | flops 1073741824 | bytes 4194304 | tf_op jit(solution)/shard_map/pallas_call | solution.py:220
  106.4 8.4 %all_to_all.20 = f32[4,2,64,128]{3,2,1,0:T(8,128)S(1)} all-to-all(f32[4,2,64,128]{3,2,1,0:T(8,128)S(1)} %pad_maximum_fusion), channel_id=1, replica_groups=mesh['freq'=4,'lat'=8] {'freq'}, dimensions={0} | all-to-all | bytes 524288 | tf_op jit(solution)/shard_map/all_to_all | solution.py:423
  (75 shorter events, 13.8 us)
Async XLA Ops:
  5.6 9.7 %copy-start.13 = (s32[2,64,512]{2,1,0:T(8,128)S(1)}, s32[2,64,512]{2,1,0:T(8,128)}, u32[]{:S(2)}) copy-start(s32[2,64,512]{2,1,0:T(8,128)} %param.19) | copy-start | bytes 786436
  7.0 9.8 %copy-start.14 = (f32[2,8]{1,0:T(2,128)S(1)}, f32[2,8]{1,0:T(2,128)}, u32[]{:S(2)}) copy-start(f32[2,8]{1,0:T(2,128)} %param.18) | copy-start | bytes 196
  8.0 16.3 %all-to-all-start = ((f32[32,1,704]{2,1,0:T(1,128)}), f32[32,1,704]{2,1,0:T(1,128)S(1)}, u32[]{:S(2)}, u32[]{:S(2)}) async-start(f32[32,1,704]{2,1,0:T(1,128)} %reshape.374), calls=%async_computation | async-start | bytes 196608 | tf_op jit(solution)/shard_map/all_to_all | solution.py:323
  37.1 7.1 %all-to-all-start.1 = ((f32[4,1,1024]{2,1,0:T(1,128)}), f32[4,1,1024]{2,1,0:T(1,128)S(1)}, u32[]{:S(2)}, u32[]{:S(2)}) async-start(f32[4,1,1024]{2,1,0:T(1,128)} %reshape.376), calls=%async_computation.1 | async-start | bytes 32768 | tf_op jit(solution)/shard_map/all_to_all | solution.py:333
  40.4 23.1 %copy-start.2 = (f32[1024,128]{1,0:T(8,128)S(1)}, f32[1024,128]{1,0:T(8,128)}, u32[]{:S(2)}) copy-start(f32[1024,128]{1,0:T(8,128)} %constant.147.clone.table_ref) | copy-start | bytes 1572868
  45.0 18.5 %copy-start = (bf16[2,512,512]{2,1,0:T(8,128)(2,1)S(1)}, bf16[2,512,512]{2,1,0:T(8,128)(2,1)}, u32[]{:S(2)}) copy-start(bf16[2,512,512]{2,1,0:T(8,128)(2,1)} %constant.144.clone.high_ref) | copy-start | bytes 3145732
  45.0 18.5 %copy-start.1 = (bf16[2,512,512]{2,1,0:T(8,128)(2,1)S(1)}, bf16[2,512,512]{2,1,0:T(8,128)(2,1)}, u32[]{:S(2)}) copy-start(bf16[2,512,512]{2,1,0:T(8,128)(2,1)} %constant.145.clone.low_ref) | copy-start | bytes 3145732
  48.6 1.0 copy-start.4
  50.7 12.7 %all-to-all-start.2 = ((f32[8,16,128]{2,1,0:T(8,128)}), f32[8,16,128]{2,1,0:T(8,128)S(1)}, u32[]{:S(2)}, u32[]{:S(2)}) async-start(f32[8,16,128]{2,1,0:T(8,128)} %shard_map.133), calls=%async_computation.2 | async-start | bytes 131072 | tf_op jit(solution)/shard_map/all_to_all | solution.py:388
  63.4 1.0 copy-start.5
  64.5 1.0 copy-start.6
  67.2 11.1 %copy-start.12 = (s32[64,512]{1,0:T(8,128)S(1)}, s32[64,512]{1,0:T(8,128)}, u32[]{:S(2)}) copy-start(s32[64,512]{1,0:T(8,128)} %get-tuple-element.17.group_ref) | copy-start | bytes 393220
  78.3 10.4 %copy-start.3 = (f32[2,512,128]{2,1,0:T(8,128)S(1)}, f32[2,512,128]{2,1,0:T(8,128)}, u32[]{:S(2)}) copy-start(f32[2,512,128]{2,1,0:T(8,128)} %get-tuple-element.27.even_ref) | copy-start | bytes 1572868
  80.1 8.7 %copy-start.9 = (f32[1,64,512]{2,1,0:T(8,128)}, f32[1,64,512]{2,1,0:T(8,128)S(1)}, u32[]{:S(2)}) copy-start(f32[1,64,512]{2,1,0:T(8,128)S(1)} %get-tuple-element.5) | copy-start | bytes 393220
  90.8 12.6 %copy-start.7 = (f32[64,512]{1,0:T(8,128)S(1)}, f32[64,512]{1,0:T(8,128)}, u32[]{:S(2)}) copy-start(f32[64,512]{1,0:T(8,128)} %get-tuple-element.20.sin_ref) | copy-start | bytes 393220
  90.8 12.6 %copy-start.8 = (f32[64,512]{1,0:T(8,128)S(1)}, f32[64,512]{1,0:T(8,128)}, u32[]{:S(2)}) copy-start(f32[64,512]{1,0:T(8,128)} %get-tuple-element.21.cos_ref) | copy-start | bytes 393220
  90.8 12.6 %copy-start.11 = (s32[64,512]{1,0:T(8,128)S(1)}, s32[64,512]{1,0:T(8,128)}, u32[]{:S(2)}) copy-start(s32[64,512]{1,0:T(8,128)} %get-tuple-element.16.group_ref) | copy-start | bytes 393220
  103.5 2.8 %copy-start.10 = (f32[1,64,512]{2,1,0:T(8,128)S(1)}, f32[1,64,512]{2,1,0:T(8,128)}, u32[]{:S(2)}) copy-start(f32[1,64,512]{2,1,0:T(8,128)} %copy-done.9) | copy-start | bytes 393220
